TPU v7x, 32 devices: a whole 2x2x4 slice. The times are simulated.
32 devices in a mesh: tm: 8 (over y, x, core), sr: 4 (over z).
Axes of the slice: x: 2, y: 2, z: 4, core: 2. Of those that a mesh axis runs over, the one named last changes fastest.
Arguments:
- observations: bfloat16 [1024, 65536], P(None, ('sr', 'tm')), may hold values from -6 to 6
- loadings: float32 [65536, 128], P(('sr', 'tm')), may hold values from -0.0007324219 to 0.0007324219
- noise_precision: float32 [65536], P(('sr', 'tm')), may hold values from 0.5 to 4
- transition: float32 [128, 128], replicated, may hold values from -1 to 1, as said below
- filter_cov: float32 [128, 128], replicated, may hold values from -1 to 1, as said below
- smoother_gain: float32 [128, 128], replicated, may hold values from -1 to 1, as said below
- smoothed_cov: float32 [128, 128], replicated, may hold values from -1 to 1, as said below
Outputs:
- smoothed_factors: float32 [1024, 128], P('tm')
- new_loadings: float32 [65536, 128], P(('sr', 'tm'))
- new_transition: float32 [128, 128], replicated
Inputs may be any that keep to these rules, and one draw needn't show every extreme that they name: `transition`: the spectral radius is below one. `filter_cov`: symmetric positive definite. `smoother_gain`: the spectral radius is below one. `smoothed_cov`: symmetric positive definite.
All inputs are finite; a program needn't handle non-finite values.
Results may differ from a plain program's by a relative error of at most 0.00175.
The roundings to bfloat16 on the way count: a program that leaves them out, or rounds other values in their place, can miss the bound.
Values may be sent and summed in bfloat16 or wider, within the bound.
A program may use at most 64 MiB of HBM per device.

v0:
```python
import jax
import jax.numpy as jnp
from jax import lax
from jax.sharding import PartitionSpec as P

precise = lax.Precision.HIGHEST


def carried_in(part, axis, combine, identity, reverse):
    count = lax.axis_size(axis)
    place = lax.axis_index(axis)
    ahead = count - 1 - place if reverse else place
    gathered = jax.tree.map(lambda a: lax.all_gather(a, axis), part)
    state = jax.tree.map(lambda a, e: jnp.zeros_like(a) + jnp.asarray(e, a.dtype), part, identity)

    def one(hop, state):
        source = count - 1 - hop if reverse else hop
        return combine(
            state, jax.tree.map(lambda a: lax.dynamic_index_in_dim(a, source, 0, False), gathered)
        )

    return lax.fori_loop(0, ahead, one, state)


def shifted(value, axis, steps):
    count = lax.axis_size(axis)
    leading, last = (max(0, -steps), min(count, count - steps))
    return lax.ppermute(value, axis, [(source, source + steps) for source in range(leading, last)])


def dot_high(left, right):
    return jnp.dot(left, right, precision=precise, preferred_element_type=jnp.float32)


def matrix_power(matrix, exponent):
    result = jnp.eye(matrix.shape[0], dtype=jnp.float32)
    square = matrix
    remain = exponent
    while remain > 0:
        if remain % 2 == 1:
            result = dot_high(result, square)
        remain = remain // 2
        if remain > 0:
            square = dot_high(square, square)
    return result


def block_prefix(inputs, matrix):
    length = inputs.shape[0]
    width = inputs.shape[1]
    totals = inputs
    raised = matrix
    offset = 1
    while offset < length:
        moved = jnp.concatenate(
            [jnp.zeros((offset, width), jnp.float32), totals[: length - offset]], axis=0
        )
        totals = totals + dot_high(moved, raised.T)
        offset = offset * 2
        if offset < length:
            raised = dot_high(raised, raised)
    return totals


def propagate(start, matrix, length):
    carried = dot_high(matrix, start)[None, :]
    raised = matrix
    while carried.shape[0] < length:
        carried = jnp.concatenate([carried, dot_high(carried, raised.T)], axis=0)
        raised = dot_high(raised, raised)
    return carried


def compose(earlier, later):
    return (dot_high(later[0], earlier[0]), dot_high(later[0], earlier[1]) + later[1])


def local(
    observations, loadings, noise_precision, transition, filter_cov, smoother_gain, smoothed_cov
):
    blocks = lax.axis_size("tm")
    position = lax.axis_index("tm")
    width = transition.shape[0]
    steps_dev = observations.shape[0] // blocks
    scaled = (noise_precision[:, None] * loadings).astype(jnp.bfloat16)
    window = observations
    partial_value = lax.psum_scatter(
        jnp.dot(window, scaled, preferred_element_type=jnp.float32),
        "tm",
        scatter_dimension=0,
        tiled=True,
    )
    info_part = dot_high(loadings.T, noise_precision[:, None] * loadings)
    proj = lax.psum(partial_value, "sr")
    info = lax.psum(info_part, ("tm", "sr"))
    closed = transition - dot_high(filter_cov, dot_high(info, transition))
    inputs = dot_high(proj, filter_cov.T)
    local_filter = block_prefix(inputs, closed)
    whole_filter = matrix_power(closed, steps_dev)
    identity_pair = (jnp.eye(width, dtype=jnp.float32), jnp.zeros((width,), jnp.float32))
    entering = carried_in(
        (whole_filter, local_filter[steps_dev - 1]), "tm", compose, identity_pair, False
    )[1]
    filtered = local_filter + propagate(entering, closed, steps_dev)
    coupled = dot_high(smoother_gain, transition)
    global_rows = position * steps_dev + jnp.arange(steps_dev, dtype=jnp.int32)
    final_row = (global_rows == steps_dev * blocks - 1)[:, None]
    back = jnp.where(final_row, filtered, filtered - dot_high(filtered, coupled.T))
    local_smooth = block_prefix(back[::-1], smoother_gain)[::-1]
    whole_smooth = matrix_power(smoother_gain, steps_dev)
    arriving = carried_in((whole_smooth, local_smooth[0]), "tm", compose, identity_pair, True)[1]
    smoothed = local_smooth + propagate(arriving, smoother_gain, steps_dev)[::-1]
    factors_b = smoothed.astype(jnp.bfloat16)
    prior_row = shifted(smoothed[steps_dev - 1 :], "tm", 1)
    lag_rows = jnp.concatenate([prior_row, smoothed[: steps_dev - 1]], axis=0)
    kept_rows = jnp.where(final_row, 0.0, smoothed)
    total_part = dot_high(smoothed.T, smoothed)
    previous_part = dot_high(kept_rows.T, kept_rows)
    lagged_part = dot_high(smoothed.T, lag_rows)
    total, previous, lagged = lax.psum((total_part, previous_part, lagged_part), "tm")
    length = steps_dev * blocks
    total = total + length * smoothed_cov
    previous = previous + (length - 1) * smoothed_cov
    lagged = lagged + (length - 1) * dot_high(smoothed_cov, smoother_gain.T)
    window = observations
    cross = jnp.einsum(
        "ts,tk->sk",
        window,
        lax.all_gather(factors_b, "tm", axis=0, tiled=True),
        preferred_element_type=jnp.float32,
    )
    total_factor = jnp.linalg.cholesky(total)
    new_loadings = jax.scipy.linalg.cho_solve((total_factor, True), cross.T).T
    previous_factor = jnp.linalg.cholesky(previous)
    new_transition = jax.scipy.linalg.cho_solve((previous_factor, True), lagged.T).T
    return (smoothed, new_loadings, new_transition)


def solution(mesh):
    in_specs = (P(None, ("sr", "tm")), P(("sr", "tm"), None), P(("sr", "tm")), P(), P(), P(), P())
    out_specs = (P("tm", None), P(("sr", "tm"), None), P())
    return jax.shard_map(local, mesh=mesh, in_specs=in_specs, out_specs=out_specs, check_vma=False)
```

profile of v0, /device:TPU:0, one launch (start us, length us, event | category | flops | bytes accessed | tf_op | source)
XLA Modules:
  0.0 331.9 jit_solution(2547815003200978211)
XLA Ops:
  8.1 4.4 %fusion.13 = f32[128,128]{0,1:T(8,128)} fusion(f32[2048,128]{1,0:T(8,128)} %param.13, f32[2048]{0:T(1024)} %param.14), kind=kOutput, calls=%fused_computation.18 | convolution fusion | flops 402915328 | bytes 1122304 | tf_op jit(solution)/shard_map/dot_general | solution.py:32
  12.6 5.3 %convolution_bitcast_fusion.2 = f32[1024,128]{0,1:T(8,128)} fusion(bf16[1024,2048]{1,0:T(8,128)(2,1)} %param.12, f32[2048,128]{1,0:T(8,128)} %param.13, f32[2048]{0:T(1024)} %param.14), kind=kOutput, calls=%fused_computation.15 | convolution fusion | flops 537395200 | bytes 5775360 | tf_op jit(solution)/shard_map/dot_general | solution.py:88
  20.3 11.4 %all-gather.1 = f32[1024,128]{1,0:T(8,128)S(1)} all-gather(f32[128,128]{1,0:T(8,128)S(1)} %fusion.46), channel_id=3, replica_groups=mesh['tm'=8,'sr'=4] {'tm'}, dimensions={0}, use_global_device_ids=true | all-gather | bytes 589824 | tf_op jit(solution)/shard_map/all_gather | solution.py:13
  31.7 105.7 %all-reduce.21.cloned.1.call-done = f32[128,128]{0,1:T(8,128)} async-done(((f32[128,128]{0,1:T(8,128)}), f32[128,128]{0,1:T(8,128)}) %all-reduce.21.cloned.1.call-update) | async-done | bytes 65552 | tf_op jit(solution)/shard_map/psum | solution.py:95
  137.3 1.1 fusion.125
  138.5 0.3 fusion.16
  140.6 10.4 %all-gather = f32[1024,128]{1,0:T(8,128)S(1)} all-gather(f32[128,128]{1,0:T(8,128)S(1)} %fusion.47), channel_id=2, replica_groups=mesh['tm'=8,'sr'=4] {'tm'}, dimensions={0}, use_global_device_ids=true | all-gather | bytes 589824 | tf_op jit(solution)/shard_map/all_gather | solution.py:13
  151.0 25.0 %all-reduce.19.cloned.1.call-done = f32[128,128]{0,1:T(8,128)} async-done(((f32[128,128]{0,1:T(8,128)}), f32[128,128]{0,1:T(8,128)}) %all-reduce.19.cloned.1.call-update) | async-done | bytes 65552 | tf_op jit(solution)/shard_map/psum | solution.py:94
  176.0 1.1 fusion.124
  179.0 8.8 %all-gather.2 = f32[8,1,128]{2,1,0:T(1,128)S(1)} all-gather(f32[1,1,128]{2,1,0:T(1,128)S(1)} %slice_bitcast_fusion.1), channel_id=1, replica_groups=mesh['tm'=8,'sr'=4] {'tm'}, dimensions={0}, use_global_device_ids=true | all-gather | bytes 4608 | tf_op jit(solution)/shard_map/all_gather | solution.py:13
  191.8 9.7 %all-gather.3 = f32[8,1,128]{2,1,0:T(1,128)S(1)} all-gather(f32[1,1,128]{2,1,0:T(1,128)S(1)} %slice_bitcast_fusion), channel_id=1, replica_groups=mesh['tm'=8,'sr'=4] {'tm'}, dimensions={0}, use_global_device_ids=true | all-gather | bytes 4608 | tf_op jit(solution)/shard_map/all_gather | solution.py:13
  201.5 1.6 while.27
  205.1 1.0 fusion.36
  206.1 0.9 fusion.147
  207.0 2.0 collective-permute-start
  209.0 8.7 %all_gather.27 = bf16[1024,128]{1,0:T(8,128)(2,1)S(1)} all-gather(bf16[128,128]{1,0:T(8,128)(2,1)S(1)} %get-tuple-element.157), channel_id=1, replica_groups=mesh['tm'=8,'sr'=4] {'tm'}, dimensions={0}, use_global_device_ids=true | all-gather | bytes 294912 | tf_op jit(solution)/shard_map/all_gather | solution.py:129
  217.7 0.9 fusion.21
  218.7 2.9 fusion.148
  221.6 49.8 %all-reduce.23.cloned.1.call-done = (f32[128,128]{0,1:T(8,128)}, f32[128,128]{0,1:T(8,128)}, f32[128,128]{0,1:T(8,128)}) async-done(((f32[128,128]{0,1:T(8,128)}, f32[128,128]{0,1:T(8,128)}, f32[128,128]{0,1:T(8,128)}), (f32[128,128]{0,1:T(8,128)}, f32[128,128]{0,1:T(8,128)}, f32[128,128]{0,1:T(8,128)})) %all-reduce.23.cloned.1.call-update) | async-done | bytes 196624 | tf_op jit(solution)/shard_map/psum | solution.py:120
  271.4 0.9 multiply_add_fusion
  272.5 11.7 %cholesky.55 = f32[128,128]{1,0:T(8,128)S(1)} custom-call(f32[128,128]{1,0:T(8,128)S(1)} %get-tuple-element.161), custom_call_target="Cholesky" | custom-call | tf_op jit(solution)/shard_map/jit(cholesky)/cholesky | solution.py:134
  284.3 0.6 compare_reduce_fusion
  284.9 0.7 fusion.20
  285.6 9.8 %custom-call.17 = f32[1,128,128]{1,2,0:T(8,128)S(1)} custom-call(f32[1,128,128]{2,1,0:T(8,128)S(1)} %fusion.20), custom_call_target="InvertDiagBlocksLowerTriangular" | custom-call | tf_op jit(solution)/shard_map/jit(_cho_solve)/triangular_solve | solution.py:135
  295.4 1.1 fusion.27
  296.5 0.9 fusion.25
  297.4 11.7 %cholesky.44 = f32[128,128]{1,0:T(8,128)S(1)} custom-call(f32[128,128]{1,0:T(8,128)S(1)} %get-tuple-element.162), custom_call_target="Cholesky" | custom-call | tf_op jit(solution)/shard_map/jit(cholesky)/cholesky | solution.py:132
  309.2 0.6 compare_reduce_fusion.1
  309.8 0.7 fusion.19
  310.5 9.9 %custom-call.16 = f32[1,128,128]{1,2,0:T(8,128)S(1)} custom-call(f32[1,128,128]{2,1,0:T(8,128)S(1)} %fusion.19), custom_call_target="InvertDiagBlocksLowerTriangular" | custom-call | tf_op jit(solution)/shard_map/jit(_cho_solve)/triangular_solve | solution.py:133
  320.5 1.1 fusion.32
  321.5 2.8 fusion.30
  (119 shorter events, 13.9 us)
Async XLA Ops:
  8.0 10.0 %copy-start = (f32[128,128]{1,0:T(8,128)S(1)}, f32[128,128]{1,0:T(8,128)}, u32[]{:S(2)}) copy-start(f32[128,128]{1,0:T(8,128)} %param.17) | copy-start | bytes 196612
  8.0 9.9 %copy-start.2 = (f32[128,128]{1,0:T(8,128)S(1)}, f32[128,128]{1,0:T(8,128)}, u32[]{:S(2)}) copy-start(f32[128,128]{1,0:T(8,128)} %param.15) | copy-start | bytes 196612
  8.0 10.4 %copy-start.3 = (f32[128,128]{1,0:T(8,128)S(1)}, f32[128,128]{1,0:T(8,128)}, u32[]{:S(2)}) copy-start(f32[128,128]{1,0:T(8,128)} %param.18) | copy-start | bytes 196612
  8.0 129.3 %all-reduce.21.cloned.1.call-start = ((), (), s32[]{:S(2)}) async-start(), calls=%async_computation.3 | async-start | bytes 131072 | tf_op jit(solution)/shard_map/psum | solution.py:95
  12.5 126.0 %copy-start.4 = (f32[128,128]{1,0:T(8,128)S(1)}, f32[128,128]{1,0:T(8,128)}, u32[]{:S(2)}) copy-start(f32[128,128]{1,0:T(8,128)} %param.16) | copy-start | bytes 196612
  12.5 128.0 %reduce-scatter.2.cloned.1.call-start = ((), (), s32[]{:S(2)}) async-start(), calls=%async_computation.1 | async-start | bytes 589824 | tf_op jit(solution)/shard_map/reduce_scatter | solution.py:87
  17.9 158.1 %all-reduce.19.cloned.1.call-start = ((), (), s32[]{:S(2)}) async-start(), calls=%async_computation.2 | async-start | bytes 131072 | tf_op jit(solution)/shard_map/psum | solution.py:94
  140.6 130.9 %all-reduce.23.cloned.1.call-start = ((), (), s32[]{:S(2)}) async-start(), calls=%async_computation.4 | async-start | bytes 393216 | tf_op jit(solution)/shard_map/psum | solution.py:120
  205.1 105.4 %copy-start.1 = (f32[128,128]{1,0:T(8,128)}, f32[128,128]{1,0:T(8,128)S(1)}, u32[]{:S(2)}) copy-start(f32[128,128]{1,0:T(8,128)S(1)} %get-tuple-element.158) | copy-start | bytes 196612
  207.0 10.7 %collective-permute-start = (f32[1,128]{1,0:T(1,128)S(1)}, f32[1,128]{1,0:T(1,128)S(1)}, u32[]{:S(2)}, u32[]{:S(2)}) collective-permute-start(f32[1,128]{1,0:T(1,128)S(1)} %slice.121), channel_id=1, source_target_pairs={{0,4},{4,8},{8,12},{12,16},{16,20},{20,24},{24,28},{1,5},{5,9},{9,... | collective-permute-start | bytes 1544 | tf_op jit(solution)/shard_map/ppermute | solution.py:28
Sparse Core Ops, SparseCore 0:
  15.0 122.2 all-reduce.20
Sparse Core Ops, SparseCore 1:
  18.0 36.8 reduce-scatter.1
  140.6 35.2 all-reduce.18
  218.7 52.6 all-reduce.22
where the time goes:
time: 332 us
  waiting for transfers between devices  181 us (55%)
  blocking collectives  48.9 us (15%)
  other arithmetic  46.8 us (14%)
  matrix products  36.4 us (11%)
  between operations  16.2 us (5%)
    psum x1, waiting for transfers between devices, local(): info = lax.psum(info_part, ('tm', 'sr'))  106 us
    psum x1, waiting for transfers between devices, local(): lax.psum((total_part, previous_part, lagged_part), 'tm')  49.8 us
    all_gather x4, blocking collectives, carried_in(): gathered = jax.tree.map(lambda a: lax.all_gather(a, axis), part)  40.2 us
    psum x1, waiting for transfers between devices, local(): proj = lax.psum(partial_value, 'sr')  25 us
    dot_general x63, matrix products, dot_high(): jnp.dot(left, right, precision=precise, preferred_element_type=jnp.float32)  22.3 us
    another operation x3, other arithmetic, local(): previous_factor = jnp.linalg.cholesky(previous)  12.4 us
    another operation x3, other arithmetic, local(): total_factor = jnp.linalg.cholesky(total)  12.4 us
    another operation x2, other arithmetic, local(): new_loadings = jax.scipy.linalg.cho_solve((total_factor, True), cross.T).T  10.6 us
  transfers between devices with their start and end apart: 5, of which 3 were waited for; matrix products, arithmetic and copies ran while one was open for 4% of the time, Pallas kernels for 0%

commit v1 on v0

--- a/solution.py
+++ b/solution.py
@@ -91,7 +91,7 @@
         tiled=True,
     )
     info_part = dot_high(loadings.T, noise_precision[:, None] * loadings)
-    proj = lax.psum(partial_value, "sr")
+    proj = jnp.sum(lax.all_gather(partial_value, "sr"), axis=0)
     info = lax.psum(info_part, ("tm", "sr"))
     closed = transition - dot_high(filter_cov, dot_high(info, transition))
     inputs = dot_high(proj, filter_cov.T)

time: 332 us -> 321 us (0.967)
  waiting for transfers between devices: 181 us -> 156 us
  blocking collectives: 48.9 us -> 63.2 us
    psum x1 -> x0, waiting for transfers between devices: 25 us -> none  [local(): proj = lax.psum(partial_value, 'sr')]
    all_gather x0 -> x1, blocking collectives: none -> 14.3 us  [local(): proj = jnp.sum(lax.all_gather(partial_value, 'sr'), axis=0)]
  transfers between devices with their start and end apart: 5 -> 4, of which waited for: 3 -> 2; matrix products, arithmetic and copies ran while one was open for 4% -> 4% of each run, Pallas kernels for 0% -> 0%
where the time goes in v1:
time: 321 us; the launch traced here: 320 us
  waiting for transfers between devices  156 us (49%)
  blocking collectives  63.2 us (20%)
  other arithmetic  46.9 us (15%)
  matrix products  35.5 us (11%)
  between operations  16 us (5%)
    psum x1, waiting for transfers between devices, local(): info = lax.psum(info_part, ('tm', 'sr'))  106 us
    psum x1, waiting for transfers between devices, local(): lax.psum((total_part, previous_part, lagged_part), 'tm')  49.8 us
    all_gather x4, blocking collectives, carried_in(): gathered = jax.tree.map(lambda a: lax.all_gather(a, axis), part)  39.8 us
    dot_general x63, matrix products, dot_high(): jnp.dot(left, right, precision=precise, preferred_element_type=jnp.float32)  21.5 us
    all_gather x1, blocking collectives, local(): proj = jnp.sum(lax.all_gather(partial_value, 'sr'), axis=0)  14.3 us
    another operation x3, other arithmetic, local(): previous_factor = jnp.linalg.cholesky(previous)  12.4 us
    another operation x3, other arithmetic, local(): total_factor = jnp.linalg.cholesky(total)  12.4 us
    another operation x2, other arithmetic, local(): new_loadings = jax.scipy.linalg.cho_solve((total_factor, True), cross.T).T  10.6 us
  transfers between devices with their start and end apart: 4, of which 2 were waited for; matrix products, arithmetic and copies ran while one was open for 4% of the time, Pallas kernels for 0%

profile of v1, /device:TPU:0, one launch (start us, length us, event | category | flops | bytes accessed | tf_op | source)
XLA Modules:
  0.0 320.5 jit_solution(1106146978165982557)
XLA Ops:
  8.1 4.4 %fusion.13 = f32[128,128]{0,1:T(8,128)} fusion(f32[2048,128]{1,0:T(8,128)} %param.13, f32[2048]{0:T(1024)} %param.14), kind=kOutput, calls=%fused_computation.18 | convolution fusion | flops 402915328 | bytes 1122304 | tf_op jit(solution)/shard_map/dot_general | solution.py:32
  12.6 5.3 %convolution_bitcast_fusion.2 = f32[1024,128]{0,1:T(8,128)} fusion(bf16[1024,2048]{1,0:T(8,128)(2,1)} %param.12, f32[2048,128]{1,0:T(8,128)} %param.13, f32[2048]{0:T(1024)} %param.14), kind=kOutput, calls=%fused_computation.15 | convolution fusion | flops 537395200 | bytes 5775360 | tf_op jit(solution)/shard_map/dot_general | solution.py:88
  20.3 11.4 %all-gather.2 = f32[1024,128]{1,0:T(8,128)S(1)} all-gather(f32[128,128]{1,0:T(8,128)S(1)} %fusion.46), channel_id=4, replica_groups=mesh['tm'=8,'sr'=4] {'tm'}, dimensions={0}, use_global_device_ids=true | all-gather | bytes 589824 | tf_op jit(solution)/shard_map/all_gather | solution.py:13
  31.7 105.7 %all-reduce.18.cloned.1.call-done = f32[128,128]{0,1:T(8,128)} async-done(((f32[128,128]{0,1:T(8,128)}), f32[128,128]{0,1:T(8,128)}) %all-reduce.18.cloned.1.call-update) | async-done | bytes 65552 | tf_op jit(solution)/shard_map/psum | solution.py:95
  137.3 1.1 fusion.125
  138.5 0.3 fusion.16
  140.5 10.4 %all-gather.1 = f32[1024,128]{1,0:T(8,128)S(1)} all-gather(f32[128,128]{1,0:T(8,128)S(1)} %fusion.47), channel_id=3, replica_groups=mesh['tm'=8,'sr'=4] {'tm'}, dimensions={0}, use_global_device_ids=true | all-gather | bytes 589824 | tf_op jit(solution)/shard_map/all_gather | solution.py:13
  150.9 14.3 %all-gather = f32[512,128]{0,1:T(8,128)S(1)} all-gather(f32[128,128]{0,1:T(8,128)} %reduce-scatter.2.cloned.1.call-done), channel_id=2, replica_groups=mesh['tm'=8,'sr'=4] {'sr'}, dimensions={0}, use_global_device_ids=true | all-gather | bytes 327680 | tf_op jit(solution)/shard_map/all_gather | solution.py:94
  165.5 0.3 fusion.124
  167.7 8.8 %all-gather.3 = f32[8,1,128]{2,1,0:T(1,128)S(1)} all-gather(f32[1,1,128]{2,1,0:T(1,128)S(1)} %slice_bitcast_fusion.1), channel_id=1, replica_groups=mesh['tm'=8,'sr'=4] {'tm'}, dimensions={0}, use_global_device_ids=true | all-gather | bytes 4608 | tf_op jit(solution)/shard_map/all_gather | solution.py:13
  180.6 9.2 %all-gather.4 = f32[8,1,128]{2,1,0:T(1,128)S(1)} all-gather(f32[1,1,128]{2,1,0:T(1,128)S(1)} %slice_bitcast_fusion), channel_id=1, replica_groups=mesh['tm'=8,'sr'=4] {'tm'}, dimensions={0}, use_global_device_ids=true | all-gather | bytes 4608 | tf_op jit(solution)/shard_map/all_gather | solution.py:13
  189.8 1.6 while.27
  193.4 1.0 fusion.36
  194.4 0.9 fusion.147
  195.3 2.0 collective-permute-start
  197.3 9.1 %all_gather.35 = bf16[1024,128]{1,0:T(8,128)(2,1)S(1)} all-gather(bf16[128,128]{1,0:T(8,128)(2,1)S(1)} %get-tuple-element.157), channel_id=1, replica_groups=mesh['tm'=8,'sr'=4] {'tm'}, dimensions={0}, use_global_device_ids=true | all-gather | bytes 294912 | tf_op jit(solution)/shard_map/all_gather | solution.py:129
  206.5 0.9 fusion.21
  207.4 2.9 fusion.148
  210.3 49.8 %all-reduce.20.cloned.1.call-done = (f32[128,128]{0,1:T(8,128)}, f32[128,128]{0,1:T(8,128)}, f32[128,128]{0,1:T(8,128)}) async-done(((f32[128,128]{0,1:T(8,128)}, f32[128,128]{0,1:T(8,128)}, f32[128,128]{0,1:T(8,128)}), (f32[128,128]{0,1:T(8,128)}, f32[128,128]{0,1:T(8,128)}, f32[128,128]{0,1:T(8,128)})) %all-reduce.20.cloned.1.call-update) | async-done | bytes 196624 | tf_op jit(solution)/shard_map/psum | solution.py:120
  260.1 0.9 multiply_add_fusion
  261.3 11.7 %cholesky.55 = f32[128,128]{1,0:T(8,128)S(1)} custom-call(f32[128,128]{1,0:T(8,128)S(1)} %get-tuple-element.161), custom_call_target="Cholesky" | custom-call | tf_op jit(solution)/shard_map/jit(cholesky)/cholesky | solution.py:134
  273.0 0.6 compare_reduce_fusion
  273.6 0.7 fusion.20
  274.3 9.8 %custom-call.17 = f32[1,128,128]{1,2,0:T(8,128)S(1)} custom-call(f32[1,128,128]{2,1,0:T(8,128)S(1)} %fusion.20), custom_call_target="InvertDiagBlocksLowerTriangular" | custom-call | tf_op jit(solution)/shard_map/jit(_cho_solve)/triangular_solve | solution.py:135
  284.1 1.1 fusion.27
  285.3 0.9 fusion.25
  286.2 11.7 %cholesky.44 = f32[128,128]{1,0:T(8,128)S(1)} custom-call(f32[128,128]{1,0:T(8,128)S(1)} %get-tuple-element.162), custom_call_target="Cholesky" | custom-call | tf_op jit(solution)/shard_map/jit(cholesky)/cholesky | solution.py:132
  297.9 0.6 compare_reduce_fusion.1
  298.6 0.7 fusion.19
  299.2 9.9 %custom-call.16 = f32[1,128,128]{1,2,0:T(8,128)S(1)} custom-call(f32[1,128,128]{2,1,0:T(8,128)S(1)} %fusion.19), custom_call_target="InvertDiagBlocksLowerTriangular" | custom-call | tf_op jit(solution)/shard_map/jit(_cho_solve)/triangular_solve | solution.py:133
  309.2 1.1 fusion.32
  310.2 2.8 fusion.30
  (119 shorter events, 14.1 us)
Async XLA Ops:
  8.0 10.0 %copy-start = (f32[128,128]{1,0:T(8,128)S(1)}, f32[128,128]{1,0:T(8,128)}, u32[]{:S(2)}) copy-start(f32[128,128]{1,0:T(8,128)} %param.17) | copy-start | bytes 196612
  8.0 9.9 %copy-start.2 = (f32[128,128]{1,0:T(8,128)S(1)}, f32[128,128]{1,0:T(8,128)}, u32[]{:S(2)}) copy-start(f32[128,128]{1,0:T(8,128)} %param.15) | copy-start | bytes 196612
  8.0 10.4 %copy-start.3 = (f32[128,128]{1,0:T(8,128)S(1)}, f32[128,128]{1,0:T(8,128)}, u32[]{:S(2)}) copy-start(f32[128,128]{1,0:T(8,128)} %param.18) | copy-start | bytes 196612
  8.0 129.3 %all-reduce.18.cloned.1.call-start = ((), (), s32[]{:S(2)}) async-start(), calls=%async_computation.2 | async-start | bytes 131072 | tf_op jit(solution)/shard_map/psum | solution.py:95
  12.5 126.0 %copy-start.4 = (f32[128,128]{1,0:T(8,128)S(1)}, f32[128,128]{1,0:T(8,128)}, u32[]{:S(2)}) copy-start(f32[128,128]{1,0:T(8,128)} %param.16) | copy-start | bytes 196612
  12.5 138.4 %reduce-scatter.2.cloned.1.call-start = ((), (), s32[]{:S(2)}) async-start(), calls=%async_computation.1 | async-start | bytes 589824 | tf_op jit(solution)/shard_map/reduce_scatter | solution.py:87
  17.9 242.3 %all-reduce.20.cloned.1.call-start = ((), (), s32[]{:S(2)}) async-start(), calls=%async_computation.3 | async-start | bytes 393216 | tf_op jit(solution)/shard_map/psum | solution.py:120
  193.4 105.9 %copy-start.1 = (f32[128,128]{1,0:T(8,128)}, f32[128,128]{1,0:T(8,128)S(1)}, u32[]{:S(2)}) copy-start(f32[128,128]{1,0:T(8,128)S(1)} %get-tuple-element.158) | copy-start | bytes 196612
  195.3 11.2 %collective-permute-start = (f32[1,128]{1,0:T(1,128)S(1)}, f32[1,128]{1,0:T(1,128)S(1)}, u32[]{:S(2)}, u32[]{:S(2)}) collective-permute-start(f32[1,128]{1,0:T(1,128)S(1)} %slice.121), channel_id=1, source_target_pairs={{0,4},{4,8},{8,12},{12,16},{16,20},{20,24},{24,28},{1,5},{5,9},{9,... | collective-permute-start | bytes 1544 | tf_op jit(solution)/shard_map/ppermute | solution.py:28
Sparse Core Ops, SparseCore 0:
  15.0 122.2 all-reduce.17
Sparse Core Ops, SparseCore 1:
  18.0 36.8 reduce-scatter.1
  207.5 52.6 all-reduce.19
